TPU v7x, 512 devices: a whole 4x4x16 slice. The times are simulated.
512 devices in a mesh: row: 16 (over x, y), col: 32 (over z, core).
Axes of the slice: x: 4, y: 4, z: 16, core: 2. Of those that a mesh axis runs over, the one named last changes fastest.
Arguments:
- start_vector: bfloat16 [4, 2048, 2048], P(None, 'row', 'col'), may hold values from -150 to 150
- left_env: bfloat16 [5, 2048, 2048], P(None, 'row', 'col'), may hold values from -5 to 6
- right_env: bfloat16 [5, 2048, 2048], P(None, 'col', 'row'), may hold values from -5 to 6
- left_tensor: float32 [5, 5, 2, 2], replicated, may hold values from -1.5 to 2.5
- right_tensor: float32 [5, 5, 2, 2], replicated, may hold values from -1.5 to 2.5
Outputs:
- next_vector: bfloat16 [4, 2048, 2048], P(None, 'row', 'col')
- coefficients: float32 [2], replicated
All inputs are finite; a program needn't handle non-finite values.
Results may differ from a plain program's by a relative error of at most 0.023.
Values may be sent and summed in bfloat16 or wider, within the bound.
No kernel may reach another device: no remote copies, remote signals or barrier semaphores. Data moves between devices by JAX's collectives and lax.ppermute only.
A program may use at most 64 MiB of HBM per device.

v0:
```python
import jax
import jax.numpy as jnp
from jax import lax
from jax.sharding import Mesh
from jax.sharding import PartitionSpec as P

ROW = ("row_0", "row_1")
COL = ("col_0", "col_1")
ROW_COL = ("row_0", "row_1", "col_0", "col_1")
epsilon = 1e-06


def copy_for_each(x, axis):
    size = lax.axis_size(axis)
    return lax.all_to_all(jnp.broadcast_to(x[None], (size, *x.shape)), axis, 0, 0, tiled=True)


def joined_along(pieces, dim):
    pieces = jnp.moveaxis(pieces, 0, dim)
    lengths = pieces.shape
    return pieces.reshape(*lengths[:dim], lengths[dim] * lengths[dim + 1], *lengths[dim + 2 :])


def gathered_copies(x, axis, dim):
    pieces = copy_for_each(x, axis)
    return joined_along(pieces, dim)


def sum_in_order(pieces, axes, sequence):
    lengths = [lax.axis_size(a) for a in axes]
    pieces = pieces.reshape(*lengths, *pieces.shape[1:])
    pieces = pieces.transpose(*sequence, *range(len(axes), pieces.ndim))
    pieces = pieces.reshape(-1, *pieces.shape[len(axes) :])
    for k in sequence:
        pieces = lax.psum_scatter(pieces, axes[k], scatter_dimension=0, tiled=True)
    return pieces[0]


def cut_along(x, dim, size):
    lengths = x.shape
    pieces = x.reshape(*lengths[:dim], size, lengths[dim] // size, *lengths[dim + 1 :])
    return jnp.moveaxis(pieces, dim, 0)


def scatter_axes(x, axes, sequence, dim):
    size = lax.axis_size(axes)
    return sum_in_order(cut_along(x, dim, size), axes, sequence)


def by_axis(x, axes):
    for axis in axes:
        x = lax.psum(x, axis)
    return x


def coupling(left_tensor, right_tensor):
    channels = left_tensor.shape[0]
    joined = jnp.einsum(
        "wuac,uvbd->vabwcd", left_tensor, right_tensor, precision=lax.Precision.HIGHEST
    )
    return joined.reshape(channels, 4, channels, 4)


def contract_left(portion, columns):
    return jnp.einsum("wax,txb->wtba", portion, columns, preferred_element_type=jnp.float32)


def mix_channels(coupling_table, cross):
    mixed_bond = jnp.einsum(
        "vswt,wtba->vsba", coupling_table, cross, precision=lax.Precision.HIGHEST
    )
    return mixed_bond.astype(jnp.bfloat16)


def contract_right(mixed_bond, portion):
    return jnp.einsum("vsba,vbc->sac", mixed_bond, portion, preferred_element_type=jnp.float32)


def apply_hamiltonian(vector, coupling_table, panels):
    columns = gathered_copies(vector, ROW, 1)
    cross = contract_left(panels[0], columns)
    mixed_bond = mix_channels(coupling_table, cross)
    partials = contract_right(mixed_bond, panels[1])
    return scatter_axes(partials.astype(jnp.bfloat16), COL, (1, 0), 2).astype(jnp.float32)


def local_mean(former, latter, entries):
    return jnp.sum(former * latter) / entries


def body(start_vector, left_env, right_env, left_tensor, right_tensor):
    coupling_table = coupling(left_tensor, right_tensor)
    entries = float(
        start_vector.shape[0]
        * start_vector.shape[1]
        * start_vector.shape[2]
        * lax.axis_size(ROW)
        * lax.axis_size(COL)
    )
    panels = (lax.all_gather(left_env, COL, axis=2, tiled=True), gathered_copies(right_env, ROW, 2))
    base_vector = start_vector.astype(jnp.float32)
    image = apply_hamiltonian(start_vector, coupling_table, panels)
    base_square, correlation, image_square = (
        by_axis(local_mean(base_vector, base_vector, entries), ROW_COL),
        by_axis(local_mean(base_vector, image, entries), ROW_COL),
        by_axis(local_mean(image, image, entries), ROW_COL),
    )
    alpha = correlation / (base_square + epsilon)
    residual = image - alpha * base_vector
    rho = jnp.sqrt(image_square - 2.0 * alpha * correlation + alpha * alpha * base_square + epsilon)
    next_vector = (residual / rho).astype(jnp.bfloat16)
    coefficients = jnp.stack([alpha, rho])
    return (next_vector, coefficients)


def solution(mesh):
    finer = Mesh(mesh.devices.reshape(4, 4, 16, 2), ("row_0", "row_1", "col_0", "col_1"))
    in_specs = (P(None, ROW, COL), P(None, ROW, COL), P(None, COL, ROW), P(), P())
    out_specs = (P(None, ROW, COL), P())
    return jax.shard_map(body, mesh=finer, in_specs=in_specs, out_specs=out_specs, check_vma=False)
```

profile of v0, /device:TPU:1, one launch (start us, length us, event | category | flops | bytes accessed | tf_op | source)
XLA Modules:
  0.0 263.9 jit_solution(11655160880378192590)
XLA Ops:
  7.2 0.0 copy-start
  7.2 0.0 all-gather.2.cloned.1.call-start
  7.2 0.7 all-gather.2.cloned.1.call-update
  7.9 1.1 broadcast_in_dim.4
  9.0 22.4 %all_to_all.10 = bf16[16,4,128,64]{2,3,1,0:T(8,128)(2,1)S(1)} all-to-all(bf16[16,4,128,64]{2,3,1,0:T(8,128)(2,1)S(1)} %broadcast_in_dim.4), channel_id=1, replica_groups=mesh['row_0'=4,'row_1'=4,'col_0'=16,'col_1'=2] {'row_0','row_1'}, dimensions={0} | all-to-all | bytes 2097152 | tf_op jit(solution)/shard_map/all_to_all | solution.py:15
  31.4 1.4 broadcast_in_dim.5
  32.8 3.7 %all-to-all-start.1 = ((bf16[16,5,64,128]{3,2,1,0:T(8,128)(2,1)}), bf16[16,5,64,128]{3,2,1,0:T(8,128)(2,1)S(1)}, u32[]{:S(2)}, u32[]{:S(2)}) async-start(bf16[16,5,64,128]{3,2,1,0:T(8,128)(2,1)} %broadcast_in_dim.5), calls=%async_computation.1 | async-start | bytes 2621440 | tf_op jit(solution)/shard_map/all_to_all | solution.py:15
  36.5 0.0 reduce-scatter.3.cloned.1.call-start
  36.6 0.4 convolution_bitcast_fusion.1
  37.0 0.7 copy.19
  37.7 1.3 reshape.35
  39.0 14.3 %all-to-all-done.1 = bf16[16,5,64,128]{3,2,1,0:T(8,128)(2,1)S(1)} async-done(((bf16[16,5,64,128]{3,2,1,0:T(8,128)(2,1)}), bf16[16,5,64,128]{3,2,1,0:T(8,128)(2,1)S(1)}, u32[]{:S(2)}, u32[]{:S(2)}) %all-to-all-start.1) | async-done | bytes 1310752 | tf_op jit(solution)/shard_map/all_to_all | solution.py:15
  53.3 0.9 copy.22
  54.2 0.6 reshape.40
  54.8 33.2 %all-gather.2.cloned.1.call-done = bf16[5,128,2048]{1,2,0:T(8,128)(2,1)} async-done(((bf16[5,128,64]{1,2,0:T(8,128)(2,1)}), bf16[5,128,2048]{1,2,0:T(8,128)(2,1)}) %all-gather.2.cloned.1.call-update) | async-done | bytes 2621456 | tf_op jit(solution)/shard_map/all_gather | solution.py:100
  88.0 3.0 %fusion.3 = f32[5,4,64,128]{3,2,0,1:T(8,128)S(1)} fusion(bf16[5,128,2048]{1,2,0:T(8,128)(2,1)} %all-gather.2.cloned.1.call-done, bf16[4,2048,64,1]{1,2,0,3:T(8,128)(2,1)} %reshape.35), kind=kOutput, calls=%fused_computation.5 | convolution fusion | flops 671088640 | bytes 4325376 | tf_op jit(solution)/shard_map/wax,txb->wtba/dot_general | solution.py:65
  91.1 4.0 %fusion.2 = bf16[5,4,64,128]{3,0,2,1:T(8,128)(2,1)S(1)} fusion(f32[5,4,64,128]{3,2,0,1:T(8,128)S(1)} %fusion.3, f32[5,4,5,4,1]{2,3,1,0,4:T(4,128)S(1)} %bitcast.57), kind=kOutput, calls=%fused_computation.4 | convolution fusion | flops 39485440 | bytes 984640 | tf_op jit(solution)/shard_map/vswt,wtba->vsba/dot_general | solution.py:69
  95.1 1.3 bitcast_convert_fusion
  96.4 2.5 copy.24
  98.9 3.2 %copy.25 = bf16[2,16,4,128,64]{3,4,2,1,0:T(8,128)(2,1)} copy(bf16[2,16,4,128,64]{3,4,0,1,2:T(8,128)(2,1)} %bitcast.54) | data formatting | bytes 4194304 | tf_op jit(solution)/shard_map/transpose | solution.py:32
  102.1 0.0 reduce-scatter.3.cloned.1.call-update
  102.1 0.0 reduce-scatter.5.cloned.1.call-start
  102.1 17.6 %reduce-scatter.3.cloned.1.call-done = bf16[16,4,128,64]{2,3,1,0:T(8,128)(2,1)} async-done(((bf16[32,4,128,64]{2,3,1,0:T(8,128)(2,1)}), bf16[16,4,128,64]{2,3,1,0:T(8,128)(2,1)}) %reduce-scatter.3.cloned.1.call-update) | async-done | bytes 1048592 | tf_op jit(solution)/shard_map/reduce_scatter | solution.py:35
  119.8 0.0 reduce-scatter.5.cloned.1.call-update
  119.8 64.3 %reduce-scatter.5.cloned.1.call-done = bf16[1,4,128,64]{2,3,1,0:T(8,128)(2,1)} async-done(((bf16[16,4,128,64]{2,3,1,0:T(8,128)(2,1)}), bf16[1,4,128,64]{2,3,1,0:T(8,128)(2,1)}) %reduce-scatter.5.cloned.1.call-update) | async-done | bytes 65552 | tf_op jit(solution)/shard_map/reduce_scatter | solution.py:35
  184.0 1.5 fusion.10
  187.5 9.5 %all-reduce.2 = (f32[]{:T(128)}, f32[]{:T(128)}, f32[]{:T(128)}) all-reduce(f32[]{:T(128)S(6)} %div.21, f32[]{:T(128)S(6)} %div.18, f32[]{:T(128)S(6)} %div.19), channel_id=1, replica_groups=mesh['row_0'=4,'row_1'=4,'col_0'=16,'col_1'=2] {'row_0'}, use_global_device_ids=true, to_apply=%region_13.0 | all-reduce | flops 3 | bytes 24 | tf_op jit(solution)/shard_map/psum | solution.py:52
  196.9 8.5 %all-reduce.1 = (f32[]{:T(128)}, f32[]{:T(128)}, f32[]{:T(128)}) all-reduce(f32[]{:T(128)} %get-tuple-element.11, f32[]{:T(128)} %get-tuple-element.12, f32[]{:T(128)} %get-tuple-element.13), channel_id=1, replica_groups=mesh['row_0'=4,'row_1'=4,'col_0'=16,'col_1'=2] {'row_1'}, use_global_device_ids=true, to_apply=%region_14.0 | all-reduce | flops 3 | bytes 24 | tf_op jit(solution)/shard_map/psum | solution.py:52
  205.5 22.2 %all-reduce = (f32[]{:T(128)}, f32[]{:T(128)}, f32[]{:T(128)}) all-reduce(f32[]{:T(128)} %get-tuple-element.8, f32[]{:T(128)} %get-tuple-element.9, f32[]{:T(128)} %get-tuple-element.10), channel_id=1, replica_groups=mesh['row_0'=4,'row_1'=4,'col_0'=16,'col_1'=2] {'col_0'}, use_global_device_ids=true, to_apply=%region_15.0 | all-reduce | flops 3 | bytes 24 | tf_op jit(solution)/shard_map/psum | solution.py:52
  227.7 24.4 %all-reduce.3 = (f32[]{:T(128)}, f32[]{:T(128)}, f32[]{:T(128)}) all-reduce(f32[]{:T(128)} %get-tuple-element.5, f32[]{:T(128)} %get-tuple-element.6, f32[]{:T(128)} %get-tuple-element.7), channel_id=1, replica_groups=mesh['row_0'=4,'row_1'=4,'col_0'=16,'col_1'=2] {'col_1'}, use_global_device_ids=true, to_apply=%region_16.0 | all-reduce | flops 3 | bytes 24 | tf_op jit(solution)/shard_map/psum | solution.py:52
  255.3 0.6 pad_maximum_fusion
  255.8 1.5 fusion.13
  (8 shorter events, 0.0 us)
Async XLA Ops:
  7.2 29.4 %copy-start = (f32[5,5,2,2]{1,3,2,0:T(2,128)S(1)}, f32[5,5,2,2]{1,3,2,0:T(2,128)}, u32[]{:S(2)}) copy-start(f32[5,5,2,2]{1,3,2,0:T(2,128)} %param.8) | copy-start | bytes 1204
  7.2 24.2 %copy-start.2 = (bf16[5,64,128]{2,1,0:T(8,128)(2,1)S(1)}, bf16[5,64,128]{2,1,0:T(8,128)(2,1)}, u32[]{:S(2)}) copy-start(bf16[5,64,128]{2,1,0:T(8,128)(2,1)} %param.7) | copy-start | bytes 245764
  7.2 80.8 %all-gather.2.cloned.1.call-start = ((), (), s32[]{:S(2)}) async-start(), calls=%async_computation.4 | async-start | bytes 2703360 | tf_op jit(solution)/shard_map/all_gather | solution.py:100
  31.4 5.2 %copy-start.3 = (f32[5,5,2,2]{1,3,2,0:T(2,128)S(1)}, f32[5,5,2,2]{1,3,2,0:T(2,128)}, u32[]{:S(2)}) copy-start(f32[5,5,2,2]{1,3,2,0:T(2,128)} %param.9) | copy-start | bytes 1204
  32.8 20.5 %all-to-all-start.1 = ((bf16[16,5,64,128]{3,2,1,0:T(8,128)(2,1)}), bf16[16,5,64,128]{3,2,1,0:T(8,128)(2,1)S(1)}, u32[]{:S(2)}, u32[]{:S(2)}) async-start(bf16[16,5,64,128]{3,2,1,0:T(8,128)(2,1)} %broadcast_in_dim.5), calls=%async_computation.1 | async-start | bytes 2621440 | tf_op jit(solution)/shard_map/all_to_all | solution.py:15
  36.5 83.2 %reduce-scatter.3.cloned.1.call-start = ((), (), s32[]{:S(2)}) async-start(), calls=%async_computation.5 | async-start | bytes 3145728 | tf_op jit(solution)/shard_map/reduce_scatter | solution.py:35
  102.1 82.0 %copy-start.1 = (bf16[4,128,64]{1,2,0:T(8,128)(2,1)S(1)}, bf16[4,128,64]{1,2,0:T(8,128)(2,1)}, u32[]{:S(2)}) copy-start(bf16[4,128,64]{1,2,0:T(8,128)(2,1)} %param.5) | copy-start | bytes 196612
  102.1 82.0 %reduce-scatter.5.cloned.1.call-start = ((), (), s32[]{:S(2)}) async-start(), calls=%async_computation.6 | async-start | bytes 1114112 | tf_op jit(solution)/shard_map/reduce_scatter | solution.py:35
Sparse Core Ops, SparseCore 0:
  10.1 77.8 all-gather.1
  102.2 17.5 reduce-scatter.2
  122.6 61.4 reduce-scatter.4
where the time goes:
time: 264 us
  waiting for transfers between devices  130 us (49%)
  blocking collectives  87.1 us (33%)
  between operations  18.9 us (7%)
  local copies, waits for them, and re-layouts  11.7 us (4%)
  matrix products  8.74 us (3%)
  starting transfers between devices  3.82 us (1%)
  other arithmetic  3.6 us (1%)
    reduce_scatter x2, waiting for transfers between devices, sum_in_order(): pieces = lax.psum_scatter(pieces, axes[k], scatter_dimension=0, tiled=True)  81.9 us
    psum x4, blocking collectives, by_axis(): x = lax.psum(x, axis)  64.7 us
    all_gather x1, waiting for transfers between devices, body(): lax.all_gather(left_env, COL, axis=2, tiled=True)  33.2 us
    all_to_all x1, blocking collectives, copy_for_each(): lax.all_to_all(jnp.broadcast_to(x[None], (size, *x.shape)), axis, 0, 0, t...  22.4 us
    all_to_all x1, waiting for transfers between devices, copy_for_each(): lax.all_to_all(jnp.broadcast_to(x[None], (size, *x.shape)), axis, 0, 0, t...  14.3 us
  transfers between devices with their start and end apart: 4, of which 4 were waited for; matrix products, arithmetic and copies ran while one was open for 2% of the time, Pallas kernels for 0%

commit v1 on v0

--- a/solution.py
+++ b/solution.py
@@ -49,7 +49,7 @@
 
 def by_axis(x, axes):
     for axis in axes:
-        x = lax.psum(x, axis)
+        x = jnp.sum(lax.all_gather(x, axis), axis=0)
     return x
 
 

time: 264 us -> 287 us (1.087)
  local copies, waits for them, and re-layouts: 11.7 us -> 31.3 us
  other arithmetic: 3.6 us -> 10.8 us
    psum x4 -> x0, blocking collectives: 64.7 us -> none  [by_axis(): x = lax.psum(x, axis)]
    unnamed x0 -> x4, blocking collectives: none -> 62.2 us
    unnamed x8 -> x36, local copies, waits for them, and re-layouts: 0.02 us -> 19.6 us
    reduce_sum x0 -> x12, other arithmetic: none -> 7.21 us  [by_axis(): x = jnp.sum(lax.all_gather(x, axis), axis=0)]
  transfers between devices with their start and end apart: 4 -> 4, of which waited for: 4 -> 4; matrix products, arithmetic and copies ran while one was open for 2% -> 3% of each run, Pallas kernels for 0% -> 0%
where the time goes in v1:
time: 287 us; the launch traced here: 286 us
  waiting for transfers between devices  128 us (45%)
  blocking collectives  84.6 us (29%)
  local copies, waits for them, and re-layouts  31.3 us (11%)
  between operations  19 us (7%)
  other arithmetic  10.8 us (4%)
  matrix products  8.74 us (3%)
  starting transfers between devices  3.82 us (1%)
    reduce_scatter x2, waiting for transfers between devices, sum_in_order(): pieces = lax.psum_scatter(pieces, axes[k], scatter_dimension=0, tiled=True)  79.3 us
    unnamed x4, blocking collectives  62.2 us
    all_gather x1, waiting for transfers between devices, body(): lax.all_gather(left_env, COL, axis=2, tiled=True)  33.2 us
    all_to_all x1, blocking collectives, copy_for_each(): lax.all_to_all(jnp.broadcast_to(x[None], (size, *x.shape)), axis, 0, 0, t...  22.4 us
    unnamed x36, local copies, waits for them, and re-layouts  19.6 us
    all_to_all x1, waiting for transfers between devices, copy_for_each(): lax.all_to_all(jnp.broadcast_to(x[None], (size, *x.shape)), axis, 0, 0, t...  14.3 us
    reduce_sum x12, other arithmetic, by_axis(): x = jnp.sum(lax.all_gather(x, axis), axis=0)  7.21 us
  transfers between devices with their start and end apart: 4, of which 4 were waited for; matrix products, arithmetic and copies ran while one was open for 3% of the time, Pallas kernels for 0%

profile of v1, /device:TPU:1, one launch (start us, length us, event | category | flops | bytes accessed | tf_op | source)
XLA Modules:
  0.0 285.8 jit_solution(2255250919447697174)
XLA Ops:
  9.0 22.4 %all_to_all.10 = bf16[16,4,128,64]{2,3,1,0:T(8,128)(2,1)S(1)} all-to-all(bf16[16,4,128,64]{2,3,1,0:T(8,128)(2,1)S(1)} %broadcast_in_dim.4), channel_id=1, replica_groups=mesh['row_0'=4,'row_1'=4,'col_0'=16,'col_1'=2] {'row_0','row_1'}, dimensions={0} | all-to-all | bytes 2097152 | tf_op jit(solution)/shard_map/all_to_all | solution.py:15
  31.4 1.4 broadcast_in_dim.5
  32.8 3.7 %all-to-all-start.1 = ((bf16[16,5,64,128]{3,2,1,0:T(8,128)(2,1)}), bf16[16,5,64,128]{3,2,1,0:T(8,128)(2,1)S(1)}, u32[]{:S(2)}, u32[]{:S(2)}) async-start(bf16[16,5,64,128]{3,2,1,0:T(8,128)(2,1)} %broadcast_in_dim.5), calls=%async_computation.1 | async-start | bytes 2621440 | tf_op jit(solution)/shard_map/all_to_all | solution.py:15
  37.7 1.3 reshape.95
  39.0 14.3 %all-to-all-done.1 = bf16[16,5,64,128]{3,2,1,0:T(8,128)(2,1)S(1)} async-done(((bf16[16,5,64,128]{3,2,1,0:T(8,128)(2,1)}), bf16[16,5,64,128]{3,2,1,0:T(8,128)(2,1)S(1)}, u32[]{:S(2)}, u32[]{:S(2)}) %all-to-all-start.1) | async-done | bytes 1310752 | tf_op jit(solution)/shard_map/all_to_all | solution.py:15
  54.8 33.2 %all-gather.2.cloned.1.call-done = bf16[5,128,2048]{1,2,0:T(8,128)(2,1)} async-done(((bf16[5,128,64]{1,2,0:T(8,128)(2,1)}), bf16[5,128,2048]{1,2,0:T(8,128)(2,1)}) %all-gather.2.cloned.1.call-update) | async-done | bytes 2621456 | tf_op jit(solution)/shard_map/all_gather | solution.py:100
  88.0 3.0 %fusion.3 = f32[5,4,64,128]{3,2,0,1:T(8,128)S(1)} fusion(bf16[5,128,2048]{1,2,0:T(8,128)(2,1)} %all-gather.2.cloned.1.call-done, bf16[4,2048,64,1]{1,2,0,3:T(8,128)(2,1)} %reshape.95), kind=kOutput, calls=%fused_computation.5 | convolution fusion | flops 671088640 | bytes 4325376 | tf_op jit(solution)/shard_map/wax,txb->wtba/dot_general | solution.py:65
  91.1 4.0 %fusion.2 = bf16[5,4,64,128]{3,0,2,1:T(8,128)(2,1)S(1)} fusion(f32[5,4,64,128]{3,2,0,1:T(8,128)S(1)} %fusion.3, f32[5,4,5,4,1]{2,3,1,0,4:T(4,128)S(1)} %bitcast.73), kind=kOutput, calls=%fused_computation.4 | convolution fusion | flops 39485440 | bytes 984640 | tf_op jit(solution)/shard_map/vswt,wtba->vsba/dot_general | solution.py:69
  95.1 1.3 bitcast_convert_fusion
  96.4 2.5 copy.24
  98.9 3.2 %copy.25 = bf16[2,16,4,128,64]{3,4,2,1,0:T(8,128)(2,1)} copy(bf16[2,16,4,128,64]{3,4,0,1,2:T(8,128)(2,1)} %bitcast.70) | data formatting | bytes 4194304 | tf_op jit(solution)/shard_map/transpose | solution.py:32
  102.1 17.6 %reduce-scatter.3.cloned.1.call-done = bf16[16,4,128,64]{2,3,1,0:T(8,128)(2,1)} async-done(((bf16[32,4,128,64]{2,3,1,0:T(8,128)(2,1)}), bf16[16,4,128,64]{2,3,1,0:T(8,128)(2,1)}) %reduce-scatter.3.cloned.1.call-update) | async-done | bytes 1048592 | tf_op jit(solution)/shard_map/reduce_scatter | solution.py:35
  119.8 1.3 dynamic-slice
  121.1 1.3 dynamic-slice.1
  122.4 61.7 %reduce-scatter.5.cloned.1.call-done = bf16[1,4,128,64]{2,3,1,0:T(8,128)(2,1)} async-done(((bf16[16,4,128,64]{2,3,1,0:T(8,128)(2,1)}), bf16[1,4,128,64]{2,3,1,0:T(8,128)(2,1)}) %reduce-scatter.5.cloned.1.call-update) | async-done | bytes 65552 | tf_op jit(solution)/shard_map/reduce_scatter | solution.py:35
  184.0 1.5 fusion.10
  189.6 1.3 dynamic-slice.2
  190.8 8.6 %all-reduce.14 = (f32[4]{0:T(128)S(1)}, f32[4]{0:T(128)S(1)}, f32[4]{0:T(128)S(1)}) all-reduce(f32[4]{0:T(128)S(1)} %dynamic-update-slice.8, f32[4]{0:T(128)S(1)} %dynamic-update-slice, f32[4]{0:T(128)S(1)} %dynamic-update-slice.4), channel_id=1, replica_groups=mesh['row_0'=4,'row_1'=4,'col_0'=16,'col_1'=2] {'row_0'}, use_global_device_ids=true, to_apply=%add.8 | all-reduce | flops 12 | bytes 96
  200.6 1.4 dynamic-update-slice.5
  202.0 1.4 dynamic-update-slice.1
  204.0 1.4 dynamic-update-slice.9
  205.3 1.3 dynamic-slice.3
  206.6 8.2 %all-reduce.13 = (f32[4]{0:T(128)S(1)}, f32[4]{0:T(128)S(1)}, f32[4]{0:T(128)S(1)}) all-reduce(f32[4]{0:T(128)S(1)} %dynamic-update-slice.9, f32[4]{0:T(128)S(1)} %dynamic-update-slice.1, f32[4]{0:T(128)S(1)} %dynamic-update-slice.5), channel_id=1, replica_groups=mesh['row_0'=4,'row_1'=4,'col_0'=16,'col_1'=2] {'row_1'}, use_global_device_ids=true, to_apply=%add.9 | all-reduce | flops 12 | bytes 96
  216.0 1.4 dynamic-update-slice.6
  217.4 1.4 dynamic-update-slice.2
  219.4 1.4 dynamic-update-slice.10
  220.8 21.5 %all-reduce.12 = (f32[16]{0:T(128)S(1)}, f32[16]{0:T(128)S(1)}, f32[16]{0:T(128)S(1)}) all-reduce(f32[16]{0:T(128)S(1)} %dynamic-update-slice.10, f32[16]{0:T(128)S(1)} %dynamic-update-slice.2, f32[16]{0:T(128)S(1)} %dynamic-update-slice.6), channel_id=1, replica_groups=mesh['row_0'=4,'row_1'=4,'col_0'=16,'col_1'=2] {'col_0'}, use_global_device_ids=true, to_apply=%add.10 | all-reduce | flops 48 | bytes 384
  243.4 1.4 dynamic-update-slice.7
  244.8 1.4 dynamic-update-slice.3
  246.8 1.4 dynamic-update-slice.11
  248.1 23.9 %all-reduce.15 = (f32[2]{0:T(128)S(1)}, f32[2]{0:T(128)S(1)}, f32[2]{0:T(128)S(1)}) all-reduce(f32[2]{0:T(128)S(1)} %dynamic-update-slice.11, f32[2]{0:T(128)S(1)} %dynamic-update-slice.3, f32[2]{0:T(128)S(1)} %dynamic-update-slice.7), channel_id=1, replica_groups=mesh['row_0'=4,'row_1'=4,'col_0'=16,'col_1'=2] {'col_1'}, use_global_device_ids=true, to_apply=%add.11 | all-reduce | flops 6 | bytes 48
  277.7 1.5 fusion.13
  (48 shorter events, 14.5 us)
Async XLA Ops:
  7.2 29.4 %copy-start = (f32[5,5,2,2]{1,3,2,0:T(2,128)S(1)}, f32[5,5,2,2]{1,3,2,0:T(2,128)}, u32[]{:S(2)}) copy-start(f32[5,5,2,2]{1,3,2,0:T(2,128)} %param.8) | copy-start | bytes 1204
  7.2 24.2 %copy-start.2 = (bf16[5,64,128]{2,1,0:T(8,128)(2,1)S(1)}, bf16[5,64,128]{2,1,0:T(8,128)(2,1)}, u32[]{:S(2)}) copy-start(bf16[5,64,128]{2,1,0:T(8,128)(2,1)} %param.7) | copy-start | bytes 245764
  7.2 80.8 %all-gather.2.cloned.1.call-start = ((), (), s32[]{:S(2)}) async-start(), calls=%async_computation.4 | async-start | bytes 2703360 | tf_op jit(solution)/shard_map/all_gather | solution.py:100
  31.4 5.2 %copy-start.3 = (f32[5,5,2,2]{1,3,2,0:T(2,128)S(1)}, f32[5,5,2,2]{1,3,2,0:T(2,128)}, u32[]{:S(2)}) copy-start(f32[5,5,2,2]{1,3,2,0:T(2,128)} %param.9) | copy-start | bytes 1204
  32.8 20.5 %all-to-all-start.1 = ((bf16[16,5,64,128]{3,2,1,0:T(8,128)(2,1)}), bf16[16,5,64,128]{3,2,1,0:T(8,128)(2,1)S(1)}, u32[]{:S(2)}, u32[]{:S(2)}) async-start(bf16[16,5,64,128]{3,2,1,0:T(8,128)(2,1)} %broadcast_in_dim.5), calls=%async_computation.1 | async-start | bytes 2621440 | tf_op jit(solution)/shard_map/all_to_all | solution.py:15
  36.5 83.2 %reduce-scatter.3.cloned.1.call-start = ((), (), s32[]{:S(2)}) async-start(), calls=%async_computation.5 | async-start | bytes 3145728 | tf_op jit(solution)/shard_map/reduce_scatter | solution.py:35
  102.1 82.0 %copy-start.1 = (bf16[4,128,64]{1,2,0:T(8,128)(2,1)S(1)}, bf16[4,128,64]{1,2,0:T(8,128)(2,1)}, u32[]{:S(2)}) copy-start(bf16[4,128,64]{1,2,0:T(8,128)(2,1)} %param.5) | copy-start | bytes 196612
  102.1 82.0 %reduce-scatter.5.cloned.1.call-start = ((), (), s32[]{:S(2)}) async-start(), calls=%async_computation.6 | async-start | bytes 1114112 | tf_op jit(solution)/shard_map/reduce_scatter | solution.py:35
Sparse Core Ops, SparseCore 0:
  10.1 77.8 all-gather.1
  102.2 17.5 reduce-scatter.2
  122.6 61.4 reduce-scatter.4
